TPU v7x, 32 devices: a whole 2x2x4 slice. The times are simulated.
32 devices in a mesh: blk: 16 (over z, y, core), rhs: 2 (over x).
Axes of the slice: x: 2, y: 2, z: 4, core: 2. Of those that a mesh axis runs over, the one named last changes fastest.
Arguments:
- signal: bfloat16 [131072, 256], P('blk', 'rhs'), may hold values from -6 to 6
- col_factor: bfloat16 [96, 131072], P(None, 'blk'), may hold values from -0.5 to 0.5
- row_factor: bfloat16 [96, 131072], P(None, 'blk'), may hold values from -0.625 to 0.625
- level_factor: bfloat16 [4, 16, 2, 64, 48, 192], P(None, 'blk', None, 'rhs'), may hold values from -0.4375 to 0.4375
- col_leaf_sizes: int32 [16, 128], P('blk'), may hold values from 1 to 128, 8192 in all within a row
- row_leaf_sizes: int32 [16, 128], P('blk'), may hold values from 1 to 128, 8192 in all within a row
- level_order: int32 [4, 16, 128], P(None, 'blk'), may hold values from 0 to 127, each once within a row
Outputs:
- result: bfloat16 [131072, 256], P('blk', 'rhs')
Inputs may be any that keep to these rules, and one draw needn't show every extreme that they name: `col_leaf_sizes`: row d lists in order the sizes of the 128 column leaves that cover unknowns d * 8192 to (d + 1) * 8192 - 1; each row sums to 8192 and its largest entry is 128. `row_leaf_sizes`: row d lists in order the sizes of the 128 row leaves that cover unknowns d * 8192 to (d + 1) * 8192 - 1; each row sums to 8192 and its largest entry is 128. Every level_order[l, d, :] is a permutation of 0 to 127.
All inputs are finite; a program needn't handle non-finite values.
Results may differ from a plain program's by a relative error of at most 0.0076.
Values may be sent and summed in bfloat16 or wider, within the bound.
A program may use at most 128 MiB of HBM per device.

v0:
```python
import functools

import jax
import jax.numpy as jnp
from jax import lax
from jax.experimental import pallas as pl
from jax.experimental.pallas import tpu as pltpu
from jax.sharding import PartitionSpec as P

LANES = 128
ROWS = 16
CHUNKS = 2
AHEAD = 2
MESH = pl.DeviceIdType.MESH


def turn(values):
    half = values.shape[-1] // 2
    return jnp.concatenate([-values[:, half:], values[:, :half]], axis=1)


def levels_kernel(
    n, order, first_hbm, lf_hbm, coef,
    own, own_tail, far, far_tail, send, arr,
    load_sem, w_send, w_recv, a_send, a_recv,
):
    levels, _, depth, rank, width = own.shape
    blocks = coef.shape[0]
    per = blocks // n
    half = n // 2
    sources = n // 4
    step = depth // CHUNKS
    me = lax.axis_index("blk")
    col = lax.axis_index("rhs")

    def load(l):
        return pltpu.make_async_copy(lf_hbm.at[l], own.at[l], load_sem.at[l])

    load_coef = pltpu.make_async_copy(first_hbm, coef, load_sem.at[levels])
    load(0).start()
    load_coef.start()
    for l in range(1, levels):
        load(l).start()

    barrier = pltpu.get_barrier_semaphore()

    def greet(k, carry):
        peer = lax.rem(me + k, n)
        pl.semaphore_signal(barrier, inc=1, device_id=(peer, col), device_id_type=MESH)
        return carry

    lax.fori_loop(1, n, greet, 0)
    pl.semaphore_signal(barrier, inc=1, device_id=(me, 1 - col), device_id_type=MESH)

    def weight_copies(l, c):
        part = pl.ds(c * step, step)
        head = pltpu.make_async_remote_copy(
            src_ref=own.at[l, :, part, :, pl.ds(0, LANES)],
            dst_ref=far.at[l, :, part],
            send_sem=w_send.at[l, c, 0],
            recv_sem=w_recv.at[l, c, 0],
            device_id=(me, 1 - col),
            device_id_type=MESH,
        )
        tail = pltpu.make_async_remote_copy(
            src_ref=own_tail.at[l, part],
            dst_ref=far_tail.at[l, part],
            send_sem=w_send.at[l, c, 1],
            recv_sem=w_recv.at[l, c, 1],
            device_id=(me, 1 - col),
            device_id_type=MESH,
        )
        return head, tail

    def pack(l):
        def one(i, carry):
            own_tail[l, i] = jnp.concatenate(
                [own[l, 0, i, :, LANES:width], own[l, 1, i, :, LANES:width]], axis=1
            )
            return carry

        lax.fori_loop(0, depth, one, 0, unroll=4)

    def send_weights(l):
        for c in range(CHUNKS):
            for copy in weight_copies(l, c):
                copy.start()

    load(0).wait()
    pack(0)
    pl.semaphore_wait(barrier, n)
    send_weights(0)

    load_coef.wait()

    def block_copy(par, peer):
        return pltpu.make_async_remote_copy(
            src_ref=send.at[peer],
            dst_ref=arr.at[par, me],
            send_sem=a_send.at[peer],
            recv_sem=a_recv.at[par, me],
            device_id=(peer, col),
            device_id_type=MESH,
        )

    def arrival(par, source):
        return pltpu.make_async_remote_copy(
            src_ref=send.at[source],
            dst_ref=arr.at[par, source],
            send_sem=a_send.at[source],
            recv_sem=a_recv.at[par, source],
            device_id=(source, col),
            device_id_type=MESH,
        )

    blank = jnp.zeros((2 * LANES - width, LANES), jnp.bfloat16)

    def level(l, carry):
        par = lax.rem(l, 2)

        def choose(peer):
            for q in range(per):
                send[peer, q] = coef[order[l, peer * per + q]]

        def hand_out(k, inner):
            peer = lax.rem(me + k, n)
            choose(peer)
            block_copy(par, peer).start()
            return inner

        lax.fori_loop(1, n, hand_out, 0)
        choose(me)
        mine = pltpu.make_async_copy(send.at[me], arr.at[par, me], a_recv.at[par, me])
        mine.start()

        @pl.when(l == 0)
        def _():
            for later in range(1, levels):
                load(later).wait()
                pack(later)
            for later in range(1, AHEAD):
                send_weights(later)

        @pl.when(l + AHEAD < levels + 0)
        def _():
            send_weights(l + AHEAD)

        def combine(s, at, head, tail):
            arrival(par, s).wait_recv()
            arrival(par, s + half).wait_recv()
            for q in range(per):
                i = at * per + q
                x = arr[par, s, q]
                y = arr[par, s + half, q]
                jx = turn(x)
                jy = turn(y)
                rest = tail[l, i]
                upper = jnp.concatenate([head(0, i), rest], axis=1)
                lower = jnp.concatenate([head(1, i), rest], axis=1)
                cut = LANES - 2 * rank
                over = jnp.concatenate([x, jx, y, jy, blank], axis=0)
                under = jnp.concatenate([y, jy, x[:cut], blank, x[cut:], jx], axis=0)
                coef[s * per + q] = jnp.dot(
                    upper, over, preferred_element_type=jnp.float32
                ).astype(jnp.bfloat16)
                coef[(s + half) * per + q] = jnp.dot(
                    lower, under, preferred_element_type=jnp.float32
                ).astype(jnp.bfloat16)

        def near(k, inner):
            combine(col * sources + k, k, lambda h, i: own[l, h, i, :, :LANES], own_tail)
            return inner

        lax.fori_loop(0, sources, near, 0)

        def distant(k, inner):
            combine((1 - col) * sources + k, k, lambda h, i: far[l, h, i], far_tail)
            return inner

        for c in range(CHUNKS):
            for copy in weight_copies(l, c):
                copy.wait_recv()
            lax.fori_loop(c * (sources // CHUNKS), (c + 1) * (sources // CHUNKS), distant, 0)

        def sent(k, inner):
            block_copy(par, lax.rem(me + k, n)).wait_send()
            return inner

        lax.fori_loop(1, n, sent, 0)
        return carry

    lax.fori_loop(0, levels, level, 0)
    for l in range(levels):
        for c in range(CHUNKS):
            for copy in weight_copies(l, c):
                copy.wait_send()


def leaves_kernel(sizes, sig, cf, coef):
    blocks, rank, _ = coef.shape
    points = sig.shape[0]
    window = 2 * LANES
    lane = lax.broadcasted_iota(jnp.int32, (1, window), 1)

    def leaf(b, start):
        end = start + sizes[0, b]
        base = jnp.minimum(start // LANES * LANES, points - window)
        base = pl.multiple_of(base, LANES)
        inside = jnp.logical_and(lane >= start - base, lane < end - base)
        keep = jnp.where(inside, 1.0, 0.0).astype(jnp.bfloat16)
        weights = cf[:, pl.ds(base, window)] * keep
        sums = jnp.dot(weights, sig[pl.ds(base, window), :], preferred_element_type=jnp.float32)
        coef[b] = (sums[:rank] + turn(sums[rank:])).astype(jnp.bfloat16)
        return end

    lax.fori_loop(0, blocks, leaf, jnp.int32(0), unroll=4)


def rows_kernel(sizes, coef, rf, out_hbm, flipped, out, sem):
    blocks, rank, _ = coef.shape
    points = rf.shape[1]
    window = LANES + ROWS

    def flip(c, carry):
        base = pl.multiple_of(c * LANES, LANES)
        flipped[pl.ds(base, LANES), :] = rf[:, pl.ds(base, LANES)].T
        return carry

    lax.fori_loop(0, points // LANES, flip, 0, unroll=4)
    row = lax.broadcasted_iota(jnp.int32, (ROWS, LANES), 0)

    def leaf(b, start):
        base = pl.multiple_of(start // ROWS * ROWS, ROWS)
        values = coef[b]
        pair = jnp.concatenate([values, turn(values)], axis=0)
        sums = jnp.dot(flipped[pl.ds(base, window), :], pair, preferred_element_type=jnp.float32)
        before = out[pl.ds(base, ROWS), :].astype(jnp.float32)
        top = jnp.where(row < start - base, before, sums[:ROWS])
        out[pl.ds(base, ROWS), :] = top.astype(jnp.bfloat16)
        out[pl.ds(base + ROWS, LANES), :] = sums[ROWS:].astype(jnp.bfloat16)
        return start + sizes[0, b]

    lax.fori_loop(0, blocks, leaf, jnp.int32(0), unroll=4)
    copy = pltpu.make_async_copy(out.at[pl.ds(0, points)], out_hbm, sem)
    copy.start()
    copy.wait()


def local(
    n, signal, col_factor, row_factor, level_factor, col_leaf_sizes, row_leaf_sizes, level_order
):
    levels, _, halves, depth, rank, width = level_factor.shape
    blocks = col_leaf_sizes.shape[1]
    points, columns = signal.shape
    bf16 = jnp.bfloat16
    smem = pl.BlockSpec(memory_space=pltpu.SMEM)
    vmem = pl.BlockSpec(memory_space=pltpu.VMEM)
    anywhere = pl.BlockSpec(memory_space=pl.ANY)
    first = pl.pallas_call(
        leaves_kernel,
        out_shape=jax.ShapeDtypeStruct((blocks, row_factor.shape[0] // 2, columns), bf16),
        in_specs=[smem, vmem, vmem],
        out_specs=vmem,
        compiler_params=pltpu.CompilerParams(vmem_limit_bytes=32 << 20),
        name="leaves",
    )(col_leaf_sizes, signal, col_factor)
    factors = level_factor.reshape(levels, halves, depth, rank, width)
    coefficients = pl.pallas_call(
        functools.partial(levels_kernel, n),
        out_shape=jax.ShapeDtypeStruct((blocks, rank, columns), bf16),
        in_specs=[smem, anywhere, anywhere],
        out_specs=vmem,
        scratch_shapes=[
            pltpu.VMEM((levels, halves, depth, rank, width), bf16),
            pltpu.VMEM((levels, depth, rank, LANES), bf16),
            pltpu.VMEM((levels, halves, depth, rank, LANES), bf16),
            pltpu.VMEM((levels, depth, rank, LANES), bf16),
            pltpu.VMEM((n, blocks // n, rank, columns), bf16),
            pltpu.VMEM((2, n, blocks // n, rank, columns), bf16),
            pltpu.SemaphoreType.DMA((levels + 1,)),
            pltpu.SemaphoreType.DMA((levels, CHUNKS, 2)),
            pltpu.SemaphoreType.DMA((levels, CHUNKS, 2)),
            pltpu.SemaphoreType.DMA((n,)),
            pltpu.SemaphoreType.DMA((2, n)),
        ],
        compiler_params=pltpu.CompilerParams(
            collective_id=0, has_side_effects=True, vmem_limit_bytes=48 << 20
        ),
        name="levels",
    )(level_order.reshape(levels, blocks), first, factors)
    return pl.pallas_call(
        rows_kernel,
        out_shape=jax.ShapeDtypeStruct((points, columns), bf16),
        in_specs=[smem, vmem, vmem],
        out_specs=anywhere,
        scratch_shapes=[
            pltpu.VMEM((points + LANES + ROWS, 2 * rank), bf16),
            pltpu.VMEM((points + LANES + ROWS, columns), bf16),
            pltpu.SemaphoreType.DMA(()),
        ],
        compiler_params=pltpu.CompilerParams(vmem_limit_bytes=40 << 20),
        name="rows",
    )(row_leaf_sizes, coefficients, row_factor)


def solution(mesh):
    in_specs = (
        P("blk", "rhs"),
        P(None, "blk"),
        P(None, "blk"),
        P(None, "blk", None, "rhs", None, None),
        P("blk", None),
        P("blk", None),
        P(None, "blk", None),
    )
    return jax.shard_map(
        functools.partial(local, mesh.shape["blk"]),
        mesh=mesh, in_specs=in_specs, out_specs=P("blk", "rhs"), check_vma=False,
    )
```

profile of v0, /device:TPU:21, one launch (start us, length us, event | category | flops | bytes accessed | tf_op | source)
XLA Modules:
  0.0 185.4 jit_solution(6663253515265599790)
XLA Ops:
  0.0 0.0 copy-start
  0.0 1.6 copy-done
  1.6 0.0 copy-start.1
  1.6 1.4 copy-done.1
  3.0 0.0 copy-start.4
  3.0 0.7 copy-done.4
  3.7 0.0 copy-start.3
  3.7 10.0 %leaves.1.first_hbm = bf16[128,48,128]{2,1,0:T(8,128)(2,1)S(1)} custom-call(s32[1,128]{1,0:T(1,128)S(1)} %copy-done.4, bf16[8192,128]{1,0:T(8,128)(2,1)S(1)} %copy-done, bf16[96,8192]{1,0:T(8,128)(2,1)S(1)} %copy-done.1), custom_call_target="tpu_custom_call" | custom-call | tf_op jit(solution)/shard_map/leaves/pallas_call | solution.py:259
  13.6 0.0 copy-done.3
  13.6 0.0 copy-start.2
  13.6 0.0 copy-start.5
  13.7 158.9 %levels.1.coef = bf16[128,48,128]{2,1,0:T(8,128)(2,1)S(1)} custom-call(s32[4,128]{1,0:T(4,128)S(1)} %bitcast.2, bf16[128,48,128]{2,1,0:T(8,128)(2,1)S(1)} %leaves.1.first_hbm, bf16[4,2,32,48,192]{4,3,2,1,0:T(8,128)(2,1)} %bitcast.3), custom_call_target="tpu_custom_call" | custom-call | tf_op jit(solution)/shard_map/levels/pallas_call | solution.py:268
  172.5 0.0 copy-done.2
  172.6 0.0 copy-done.5
  172.6 12.8 %rows.1 = bf16[8192,128]{1,0:T(8,128)(2,1)} custom-call(s32[1,128]{1,0:T(1,128)S(1)} %copy-done.5, bf16[128,48,128]{2,1,0:T(8,128)(2,1)S(1)} %levels.1.coef, bf16[96,8192]{1,0:T(8,128)(2,1)S(1)} %copy-done.2), custom_call_target="tpu_custom_call" | custom-call | tf_op jit(solution)/shard_map/rows/pallas_call | solution.py:291
Async XLA Ops:
  0.0 1.6 copy-start
  1.6 1.4 copy-start.1
  3.0 0.7 copy-start.4
  3.7 10.0 %copy-start.3 = (s32[4,1,128]{2,1,0:T(1,128)S(1)}, s32[4,1,128]{2,1,0:T(1,128)}, u32[]{:S(2)}) copy-start(s32[4,1,128]{2,1,0:T(1,128)} %param.13) | copy-start | bytes 6148
  13.6 158.9 %copy-start.2 = (bf16[96,8192]{1,0:T(8,128)(2,1)S(1)}, bf16[96,8192]{1,0:T(8,128)(2,1)}, u32[]{:S(2)}) copy-start(bf16[96,8192]{1,0:T(8,128)(2,1)} %rf.1) | copy-start | bytes 4718596
  13.6 158.9 %copy-start.5 = (s32[1,128]{1,0:T(1,128)S(1)}, s32[1,128]{1,0:T(1,128)}, u32[]{:S(2)}) copy-start(s32[1,128]{1,0:T(1,128)} %sizes.3) | copy-start | bytes 1540
where the time goes:
time: 186 us; the launch traced here: 185 us
  Pallas kernels  182 us (98%)
  local copies, waits for them, and re-layouts  3.67 us (2%)
    pallas_call x1, Pallas kernels, local(): pl.pallas_call(functools.partial(levels_kernel, n), out_shape=jax.ShapeDt...  159 us
    pallas_call x1, Pallas kernels, local(): pl.pallas_call(rows_kernel, out_shape=jax.ShapeDtypeStruct((points, colum...  12.8 us
    pallas_call x1, Pallas kernels, local(): pl.pallas_call(leaves_kernel, out_shape=jax.ShapeDtypeStruct((blocks, row...  9.96 us

commit v1 on v0

v1 whole, which is shorter than its diff:
```python
import functools

import jax
import jax.numpy as jnp
from jax import lax
from jax.experimental import pallas as pl
from jax.experimental.pallas import tpu as pltpu
from jax.sharding import PartitionSpec as P

LANES = 128
ROWS = 16
MESH = pl.DeviceIdType.MESH


def turn(values):
    half = values.shape[-1] // 2
    return jnp.concatenate([-values[:, half:], values[:, :half]], axis=1)


def levels_kernel(
    n, order, first_hbm, lf_hbm, rf_hbm, coef, flipped,
    head, tail, loose, rf, send, arr,
    load_sem, w_send, w_recv, a_send, a_recv,
):
    levels, _, _, depth, rank, _ = head.shape
    width = LANES + loose.shape[-1]
    blocks = coef.shape[0]
    points = rf.shape[1]
    per = blocks // n
    half = n // 2
    sources = n // 4
    me = lax.axis_index("blk")
    col = lax.axis_index("rhs")
    side = me // half
    place = lax.rem(me, half)

    def loads(l):
        return (
            pltpu.make_async_copy(
                lf_hbm.at[l, :, :, :, pl.ds(0, LANES)], head.at[l, col], load_sem.at[l, 0]
            ),
            pltpu.make_async_copy(
                lf_hbm.at[l, :, :, :, pl.ds(LANES, width - LANES)], loose.at[l], load_sem.at[l, 1]
            ),
        )

    load_coef = pltpu.make_async_copy(first_hbm, coef, load_sem.at[levels, 0])
    load_rows = pltpu.make_async_copy(rf_hbm, rf, load_sem.at[levels, 1])
    load_coef.start()
    for l in range(levels):
        for copy in loads(l):
            copy.start()
    load_rows.start()

    barrier = pltpu.get_barrier_semaphore()

    def greet(k, carry):
        peer = lax.rem(me + k, n)
        pl.semaphore_signal(barrier, inc=1, device_id=(peer, col), device_id_type=MESH)
        return carry

    lax.fori_loop(1, n, greet, 0)
    pl.semaphore_signal(barrier, inc=1, device_id=(me, 1 - col), device_id_type=MESH)

    def weight_copies(l, owner):
        return [
            pltpu.make_async_remote_copy(
                src_ref=ref.at[l, owner],
                dst_ref=ref.at[l, owner],
                send_sem=w_send.at[l, at],
                recv_sem=w_recv.at[l, at],
                device_id=(me, 1 - col),
                device_id_type=MESH,
            )
            for at, ref in enumerate((head, tail))
        ]

    def pack(l):
        def one(i, carry):
            tail[l, col, i] = jnp.concatenate([loose[l, 0, i], loose[l, 1, i]], axis=1)
            return carry

        lax.fori_loop(0, depth, one, 0, unroll=4)

    def block_copy(par, peer):
        return pltpu.make_async_remote_copy(
            src_ref=send.at[peer],
            dst_ref=arr.at[par, me],
            send_sem=a_send.at[peer],
            recv_sem=a_recv.at[par, me],
            device_id=(peer, col),
            device_id_type=MESH,
        )

    def arrival(par, source):
        return pltpu.make_async_remote_copy(
            src_ref=send.at[source],
            dst_ref=arr.at[par, source],
            send_sem=a_send.at[source],
            recv_sem=a_recv.at[par, source],
            device_id=(source, col),
            device_id_type=MESH,
        )

    def across(k):
        return (1 - side) * half + lax.rem(place + k, half)

    def beside(k):
        return side * half + lax.rem(place + k, half)

    blank = jnp.zeros((2 * LANES - width, LANES), jnp.bfloat16)

    load_coef.wait()
    pl.semaphore_wait(barrier, n)

    def level(l, carry):
        par = lax.rem(l, 2)

        def choose(peer):
            for q in range(per):
                send[peer, q] = coef[order[l, peer * per + q]]

        def hand_out(k, inner):
            choose(across(k))
            block_copy(par, across(k)).start()

            @pl.when(k > 0)
            def _():
                choose(beside(k))
                block_copy(par, beside(k)).start()

            return inner

        lax.fori_loop(0, half, hand_out, 0)
        choose(me)
        pltpu.make_async_copy(send.at[me], arr.at[par, me], a_recv.at[par, me]).start()

        @pl.when(l == 0)
        def _():
            for later in range(levels):
                for copy in loads(later):
                    copy.wait()
                pack(later)
                for copy in weight_copies(later, col):
                    copy.start()
            load_rows.wait()

            def flip(c, inner):
                base = pl.multiple_of(c * LANES, LANES)
                flipped[pl.ds(base, LANES), :] = rf[:, pl.ds(base, LANES)].T
                return inner

            lax.fori_loop(0, points // LANES, flip, 0, unroll=4)

        for copy in weight_copies(l, 1 - col):
            copy.wait_recv()

        def combine(k, inner):
            s = lax.rem(place + half - k, half)
            owner = s // sources
            at = lax.rem(s, sources) * per
            arrival(par, s).wait_recv()
            arrival(par, s + half).wait_recv()
            for q in range(per):
                i = at + q
                x = arr[par, s, q]
                y = arr[par, s + half, q]
                jx = turn(x)
                jy = turn(y)
                rest = tail[l, owner, i]
                upper = jnp.concatenate([head[l, owner, 0, i], rest], axis=1)
                lower = jnp.concatenate([head[l, owner, 1, i], rest], axis=1)
                cut = LANES - 2 * rank
                over = jnp.concatenate([x, jx, y, jy, blank], axis=0)
                under = jnp.concatenate([y, jy, x[:cut], blank, x[cut:], jx], axis=0)
                coef[s * per + q] = jnp.dot(
                    upper, over, preferred_element_type=jnp.float32
                ).astype(jnp.bfloat16)
                coef[(s + half) * per + q] = jnp.dot(
                    lower, under, preferred_element_type=jnp.float32
                ).astype(jnp.bfloat16)
            return inner

        lax.fori_loop(0, half, combine, 0)

        def sent(k, inner):
            block_copy(par, lax.rem(me + k, n)).wait_send()
            return inner

        lax.fori_loop(1, n, sent, 0)
        return carry

    lax.fori_loop(0, levels, level, 0)
    for l in range(levels):
        for copy in weight_copies(l, col):
            copy.wait_send()


def leaves_kernel(sizes, sig, cf, coef):
    blocks, rank, _ = coef.shape
    points = sig.shape[0]
    window = 2 * LANES
    lane = lax.broadcasted_iota(jnp.int32, (1, window), 1)

    def leaf(b, start):
        end = start + sizes[0, b]
        base = jnp.minimum(start // LANES * LANES, points - window)
        base = pl.multiple_of(base, LANES)
        inside = jnp.logical_and(lane >= start - base, lane < end - base)
        keep = jnp.where(inside, 1.0, 0.0).astype(jnp.bfloat16)
        weights = cf[:, pl.ds(base, window)] * keep
        sums = jnp.dot(weights, sig[pl.ds(base, window), :], preferred_element_type=jnp.float32)
        coef[b] = (sums[:rank] + turn(sums[rank:])).astype(jnp.bfloat16)
        return end

    lax.fori_loop(0, blocks, leaf, jnp.int32(0), unroll=8)


def rows_kernel(sizes, coef, flipped, out_hbm, out, sem):
    blocks, rank, _ = coef.shape
    points = out_hbm.shape[0]
    window = LANES + ROWS
    row = lax.broadcasted_iota(jnp.int32, (ROWS, LANES), 0)

    def leaf(b, start):
        base = pl.multiple_of(start // ROWS * ROWS, ROWS)
        values = coef[b]
        pair = jnp.concatenate([values, turn(values)], axis=0)
        sums = jnp.dot(flipped[pl.ds(base, window), :], pair, preferred_element_type=jnp.float32)
        before = out[pl.ds(base, ROWS), :].astype(jnp.float32)
        top = jnp.where(row < start - base, before, sums[:ROWS])
        out[pl.ds(base, ROWS), :] = top.astype(jnp.bfloat16)
        out[pl.ds(base + ROWS, LANES), :] = sums[ROWS:].astype(jnp.bfloat16)
        return start + sizes[0, b]

    lax.fori_loop(0, blocks, leaf, jnp.int32(0), unroll=8)
    copy = pltpu.make_async_copy(out.at[pl.ds(0, points)], out_hbm, sem)
    copy.start()
    copy.wait()


def local(
    n, signal, col_factor, row_factor, level_factor, col_leaf_sizes, row_leaf_sizes, level_order
):
    levels, _, halves, depth, rank, width = level_factor.shape
    blocks = col_leaf_sizes.shape[1]
    points, columns = signal.shape
    bf16 = jnp.bfloat16
    smem = pl.BlockSpec(memory_space=pltpu.SMEM)
    vmem = pl.BlockSpec(memory_space=pltpu.VMEM)
    anywhere = pl.BlockSpec(memory_space=pl.ANY)
    first = pl.pallas_call(
        leaves_kernel,
        out_shape=jax.ShapeDtypeStruct((blocks, row_factor.shape[0] // 2, columns), bf16),
        in_specs=[smem, vmem, vmem],
        out_specs=vmem,
        compiler_params=pltpu.CompilerParams(vmem_limit_bytes=32 << 20),
        name="leaves",
    )(col_leaf_sizes, signal, col_factor)
    factors = level_factor.reshape(levels, halves, depth, rank, width)
    coefficients, flipped = pl.pallas_call(
        functools.partial(levels_kernel, n),
        out_shape=(
            jax.ShapeDtypeStruct((blocks, rank, columns), bf16),
            jax.ShapeDtypeStruct((points + LANES + ROWS, 2 * rank), bf16),
        ),
        in_specs=[smem, anywhere, anywhere, anywhere],
        out_specs=(vmem, vmem),
        scratch_shapes=[
            pltpu.VMEM((levels, 2, halves, depth, rank, LANES), bf16),
            pltpu.VMEM((levels, 2, depth, rank, LANES), bf16),
            pltpu.VMEM((levels, halves, depth, rank, width - LANES), bf16),
            pltpu.VMEM((2 * rank, points), bf16),
            pltpu.VMEM((n, blocks // n, rank, columns), bf16),
            pltpu.VMEM((2, n, blocks // n, rank, columns), bf16),
            pltpu.SemaphoreType.DMA((levels + 1, 2)),
            pltpu.SemaphoreType.DMA((levels, 2)),
            pltpu.SemaphoreType.DMA((levels, 2)),
            pltpu.SemaphoreType.DMA((n,)),
            pltpu.SemaphoreType.DMA((2, n)),
        ],
        compiler_params=pltpu.CompilerParams(
            collective_id=0, has_side_effects=True, vmem_limit_bytes=48 << 20
        ),
        name="levels",
    )(level_order.reshape(levels, blocks), first, factors, row_factor)
    return pl.pallas_call(
        rows_kernel,
        out_shape=jax.ShapeDtypeStruct((points, columns), bf16),
        in_specs=[smem, vmem, vmem],
        out_specs=anywhere,
        scratch_shapes=[
            pltpu.VMEM((points + LANES + ROWS, columns), bf16),
            pltpu.SemaphoreType.DMA(()),
        ],
        compiler_params=pltpu.CompilerParams(vmem_limit_bytes=40 << 20),
        name="rows",
    )(row_leaf_sizes, coefficients, flipped)


def solution(mesh):
    in_specs = (
        P("blk", "rhs"),
        P(None, "blk"),
        P(None, "blk"),
        P(None, "blk", None, "rhs", None, None),
        P("blk", None),
        P("blk", None),
        P(None, "blk", None),
    )
    return jax.shard_map(
        functools.partial(local, mesh.shape["blk"]),
        mesh=mesh, in_specs=in_specs, out_specs=P("blk", "rhs"), check_vma=False,
    )
```

time: 186 us -> 166 us (0.89); the launches traced: 185 us -> 163 us
  Pallas kernels: 182 us -> 158 us
    pallas_call x1, Pallas kernels: 159 us -> 144 us  [local(): pl.pallas_call(functools.partial(levels_kernel, n), out_shape=(jax.ShapeD...]
    pallas_call x1, Pallas kernels: 12.8 us -> 7.84 us  [local(): pl.pallas_call(rows_kernel, out_shape=jax.ShapeDtypeStruct((points, colum...]
    pallas_call x1, Pallas kernels: 9.96 us -> 6.22 us  [local(): pl.pallas_call(leaves_kernel, out_shape=jax.ShapeDtypeStruct((blocks, row...]
    unnamed x12 -> x14, local copies, waits for them, and re-layouts: 3.67 us -> 5.26 us
where the time goes in v1:
time: 166 us; the launch traced here: 163 us
  Pallas kernels  158 us (95%)
  local copies, waits for them, and re-layouts  5.26 us (3%)
    pallas_call x1, Pallas kernels, local(): pl.pallas_call(functools.partial(levels_kernel, n), out_shape=(jax.ShapeD...  144 us
    pallas_call x1, Pallas kernels, local(): pl.pallas_call(rows_kernel, out_shape=jax.ShapeDtypeStruct((points, colum...  7.84 us
    pallas_call x1, Pallas kernels, local(): pl.pallas_call(leaves_kernel, out_shape=jax.ShapeDtypeStruct((blocks, row...  6.22 us
    unnamed x14, local copies, waits for them, and re-layouts  5.26 us

profile of v1, /device:TPU:21, one launch (start us, length us, event | category | flops | bytes accessed | tf_op | source)
XLA Modules:
  0.0 163.0 jit_solution(6600201641377261851)
XLA Ops:
  0.0 0.0 copy-start.1
  0.0 1.6 copy-done.1
  1.6 0.0 copy-start.3
  1.6 1.4 copy-done.3
  3.0 0.0 copy-start.5
  3.0 0.7 copy-done.5
  3.7 0.0 copy-start.2
  3.7 0.0 copy-start.4
  3.7 6.2 %leaves.1.first_hbm = bf16[128,48,128]{2,1,0:T(8,128)(2,1)S(1)} custom-call(s32[1,128]{1,0:T(1,128)S(1)} %copy-done.5, bf16[8192,128]{1,0:T(8,128)(2,1)S(1)} %copy-done.1, bf16[96,8192]{1,0:T(8,128)(2,1)S(1)} %copy-done.3), custom_call_target="tpu_custom_call" | custom-call | tf_op jit(solution)/shard_map/leaves/pallas_call | solution.py:252
  9.9 0.0 copy-done.2
  9.9 0.0 copy-done.4
  9.9 0.0 copy-start.6
  9.9 143.7 %levels.1 = (bf16[128,48,128]{2,1,0:T(8,128)(2,1)S(1)}, bf16[8336,96]{1,0:T(8,128)(2,1)}) custom-call(s32[4,128]{1,0:T(4,128)S(1)} %bitcast.2, bf16[128,48,128]{2,1,0:T(8,128)(2,1)S(1)} %leaves.1.first_hbm, bf16[4,2,32,48,192]{4,3,2,1,0:T(8,128)(2,1)} %bitcast.3, bf16[96,8192]{1,0:T(8,128)(2,1)S(1)} %copy-done.2), custom_call_target="tpu_custom_call" | custom-call | tf_op jit(solution)/shard_map/levels/pallas_call | solution.py:261
  153.6 0.0 copy-done.6
  153.6 0.0 copy-start
  153.6 1.6 copy-done
  155.2 7.8 %rows.1 = bf16[8192,128]{1,0:T(8,128)(2,1)} custom-call(s32[1,128]{1,0:T(1,128)S(1)} %copy-done.6, bf16[128,48,128]{2,1,0:T(8,128)(2,1)S(1)} %get-tuple-element.7.coef, bf16[8336,96]{1,0:T(8,128)(2,1)S(1)} %copy-done), custom_call_target="tpu_custom_call" | custom-call | tf_op jit(solution)/shard_map/rows/pallas_call | solution.py:287
Async XLA Ops:
  0.0 1.6 copy-start.1
  1.6 1.4 copy-start.3
  3.0 0.7 copy-start.5
  3.7 6.2 %copy-start.2 = (bf16[96,8192]{1,0:T(8,128)(2,1)S(1)}, bf16[96,8192]{1,0:T(8,128)(2,1)}, u32[]{:S(2)}) copy-start(bf16[96,8192]{1,0:T(8,128)(2,1)} %rf_hbm.1) | copy-start | bytes 4718596
  3.7 6.2 %copy-start.4 = (s32[4,1,128]{2,1,0:T(1,128)S(1)}, s32[4,1,128]{2,1,0:T(1,128)}, u32[]{:S(2)}) copy-start(s32[4,1,128]{2,1,0:T(1,128)} %param.13) | copy-start | bytes 6148
  9.9 143.7 %copy-start.6 = (s32[1,128]{1,0:T(1,128)S(1)}, s32[1,128]{1,0:T(1,128)}, u32[]{:S(2)}) copy-start(s32[1,128]{1,0:T(1,128)} %sizes.3) | copy-start | bytes 1540
  153.6 1.6 copy-start
